TPU v7x, 32 devices: a whole 2x2x4 slice. The times are simulated.
32 devices in a mesh: dp: 8 (over z, x), tp: 4 (over y, core).
Axes of the slice: x: 2, y: 2, z: 4, core: 2. Of those that a mesh axis runs over, the one named last changes fastest.
Arguments:
- gradients: bfloat16 [8, 4, 5120, 1280], P('dp', None, 'tp'), may hold values from -6 to 6
- right_factor: float32 [4, 1280, 32], replicated, may hold values from -6 to 6
- weights_before: float32 [4, 5120, 1280], P(None, 'tp', 'dp'), may hold values from -0.15625 to 0.15625
- momentum: float32 [4, 5120, 1280], P(None, 'tp', 'dp'), may hold values from -0.3125 to 0.3125
Outputs:
- new_weights: float32 [4, 5120, 1280], P(None, 'tp', 'dp')
- new_basis: float32 [4, 1280, 32], replicated
- new_momentum: float32 [4, 5120, 1280], P(None, 'tp', 'dp')
All inputs are finite; a program needn't handle non-finite values.
Results may differ from a plain program's by a relative error of at most 0.003.
Values sent between devices are 32-bit elements; how exact they have to be, the bound alone decides.
A program may use at most 64 MiB of HBM per device.

v0:
```python
import jax
import jax.numpy as jnp
from jax import lax
from jax.sharding import PartitionSpec as P

RANK = 32


def on_device(gradients, right_factor, weights_before, momentum):
    own_grads = gradients[0]
    part_left = jnp.einsum(
        "liw,lwr->lir",
        own_grads,
        right_factor.astype(jnp.bfloat16),
        preferred_element_type=jnp.float32,
    )
    left = lax.psum(part_left, "dp")
    part_gram = jnp.einsum("lir,lis->lrs", left, left, precision=lax.Precision.HIGHEST)
    small_left = left.astype(jnp.bfloat16)
    gram = lax.psum(part_gram, "tp")
    part_right = jnp.einsum(
        "liw,lir->lwr", own_grads, small_left, preferred_element_type=jnp.float32
    )
    right = lax.psum(part_right, ("dp", "tp"))
    gram = gram + 0.001 * jnp.mean(jnp.diagonal(gram, axis1=1, axis2=2), axis=1)[
        :, None, None
    ] * jnp.eye(RANK, dtype=jnp.float32)
    place = lax.axis_index("dp") * weights_before.shape[2]
    own_right = lax.dynamic_slice_in_dim(right, place, weights_before.shape[2], axis=1)
    root = jnp.linalg.cholesky(gram)
    half = lax.linalg.triangular_solve(
        root, jnp.swapaxes(own_right, 1, 2), left_side=True, lower=True
    )
    mixed = lax.linalg.triangular_solve(root, half, left_side=True, lower=True, transpose_a=True)
    change = jnp.einsum(
        "lir,lrw->liw", left, mixed, precision=lax.Precision.HIGHEST
    ) / lax.axis_size("dp")
    new_momentum = 0.8 * momentum + change
    new_weights = weights_before - 0.05 * new_momentum
    new_basis = right * lax.rsqrt(jnp.mean(right * right, axis=(1, 2), keepdims=True) + 1e-12)
    return (new_weights, new_basis, new_momentum)


def solution(mesh):
    return jax.shard_map(
        on_device,
        mesh=mesh,
        in_specs=(P("dp", None, "tp", None), P(), P(None, "tp", "dp"), P(None, "tp", "dp")),
        out_specs=(P(None, "tp", "dp"), P(), P(None, "tp", "dp")),
        check_vma=False,
    )
```

profile of v0, /device:TPU:0, one launch (start us, length us, event | category | flops | bytes accessed | tf_op | source)
XLA Modules:
  0.0 276.0 jit_solution(18249295536158250338)
XLA Ops:
  7.2 0.0 all-reduce.3.cloned.1.call-start
  7.2 9.6 %fusion.2 = f32[4,1280,32]{1,2,0:T(8,128)} fusion(bf16[1,4,1280,1280]{3,2,1,0:T(8,128)(2,1)} %param.4, f32[4,1280,32]{1,2,0:T(8,128)} %param.5), kind=kOutput, calls=%fused_computation.3 | convolution fusion | flops 419594240 | bytes 14417920 | tf_op jit(solution)/shard_map/liw,lwr->lir/dot_general | solution.py:11
  16.8 0.0 all-reduce.3.cloned.1.call-update
  16.8 0.0 all-reduce.5.cloned.1.call-start
  16.9 0.1 copy.13
  17.0 76.5 %all-reduce.3.cloned.1.call-done = f32[4,1280,32]{1,2,0:T(8,128)} async-done(((f32[4,1280,32]{1,2,0:T(8,128)}), f32[4,1280,32]{1,2,0:T(8,128)}) %all-reduce.3.cloned.1.call-update) | async-done | bytes 655376 | tf_op jit(solution)/shard_map/psum | solution.py:17
  93.4 2.0 fusion.18
  95.5 10.7 %psum.22 = f32[4,32,32]{1,2,0:T(8,128)S(1)} all-reduce(f32[4,32,32]{1,2,0:T(8,128)S(1)} %fusion.18), channel_id=1, replica_groups=mesh['dp'=8,'tp'=4] {'tp'}, use_global_device_ids=true, to_apply=%region_1.0 | all-reduce | flops 4096 | bytes 32768 | tf_op jit(solution)/shard_map/psum | solution.py:20
  106.1 0.5 copy.12
  106.7 0.7 gather_fusion
  107.4 0.1 multiply_add_fusion
  107.5 0.1 copy.14
  107.6 0.1 fusion.15
  107.7 11.7 %custom-call.9 = f32[4,32,32]{2,1,0:T(8,128)S(1)} custom-call(f32[4,32,32]{2,1,0:T(8,128)S(1)} %fusion.15), custom_call_target="Cholesky" | custom-call | tf_op jit(solution)/shard_map/jit(cholesky)/cholesky | solution.py:30
  119.4 8.1 %fusion.5 = f32[4,1280,32]{1,2,0:T(8,128)} fusion(bf16[1,4,1280,1280]{3,2,1,0:T(8,128)(2,1)} %param.4, f32[4,1280,32]{1,2,0:T(8,128)} %all-reduce.3.cloned.1.call-done), kind=kOutput, calls=%fused_computation.8 | convolution fusion | flops 419594240 | bytes 14417920 | tf_op jit(solution)/shard_map/liw,lir->lwr/dot_general | solution.py:21
  127.5 0.1 compare_reduce_fusion
  127.7 0.1 select_bitcast_fusion
  127.7 9.8 %custom-call.10 = f32[4,1,32,32]{2,3,1,0:T(8,128)S(1)} custom-call(f32[4,1,32,32]{3,2,1,0:T(8,128)S(1)} %select_bitcast_fusion), custom_call_target="InvertDiagBlocksLowerTriangular" | custom-call | tf_op jit(solution)/shard_map/triangular_solve | solution.py:34
  137.6 119.6 %all-reduce.5.cloned.1.call-done = f32[4,1280,32]{1,2,0:T(8,128)} async-done(((f32[4,1280,32]{1,2,0:T(8,128)}), f32[4,1280,32]{1,2,0:T(8,128)}) %all-reduce.5.cloned.1.call-update) | async-done | bytes 655376 | tf_op jit(solution)/shard_map/psum | solution.py:24
  257.2 1.2 multiply_reduce_fusion
  258.4 1.3 fusion.10
  259.7 0.3 fusion.12
  260.0 2.0 broadcast_multiply_fusion
  262.0 7.2 %multiply_subtract_fusion = (f32[4,1280,160]{1,2,0:T(8,128)}, f32[4,1280,160]{1,2,0:T(8,128)}) fusion(f32[4,1280,160]{1,2,0:T(8,128)} %param.6, f32[4,1280,32]{1,2,0:T(8,128)S(1)} %copy-done, f32[4,32,160]{2,1,0:T(8,128)S(1)} %fusion.12, f32[4,1280,160]{1,2,0:T(8,128)} %param.7), kind=kOutput, calls=%fused_computation.7 | convolution fusion | flops 318668800 | bytes 13844480 | tf_op jit(solution)/shard_map/lir,lrw->liw/dot_general | solution.py:35
  (11 shorter events, 0.1 us)
Async XLA Ops:
  7.2 86.3 %all-reduce.3.cloned.1.call-start = ((), (), s32[]{:S(2)}) async-start(), calls=%async_computation | async-start | bytes 1310720 | tf_op jit(solution)/shard_map/psum | solution.py:17
  16.8 240.4 %all-reduce.5.cloned.1.call-start = ((), (), s32[]{:S(2)}) async-start(), calls=%async_computation.1 | async-start | bytes 1310720 | tf_op jit(solution)/shard_map/psum | solution.py:24
  127.5 134.5 %copy-start = (f32[4,1280,32]{1,2,0:T(8,128)S(1)}, f32[4,1280,32]{1,2,0:T(8,128)}, u32[]{:S(2)}) copy-start(f32[4,1280,32]{1,2,0:T(8,128)} %all-reduce.3.cloned.1.call-done) | copy-start | bytes 1966084
Sparse Core Ops, SparseCore 0:
  16.9 76.4 all-reduce.2
  127.6 129.4 all-reduce.4
where the time goes:
time: 276 us
  waiting for transfers between devices  196 us (71%)
  matrix products  28.4 us (10%)
  other arithmetic  25.3 us (9%)
  between operations  14.1 us (5%)
  blocking collectives  10.7 us (4%)
    psum x1, waiting for transfers between devices, on_device(): right = lax.psum(part_right, ('dp', 'tp'))  120 us
    psum x1, waiting for transfers between devices, on_device(): left = lax.psum(part_left, 'dp')  76.5 us
    another operation x4, other arithmetic, on_device(): root = jnp.linalg.cholesky(gram)  11.9 us
    psum x1, blocking collectives, on_device(): gram = lax.psum(part_gram, 'tp')  10.7 us
    another operation x3, other arithmetic, on_device(): lax.linalg.triangular_solve(root, half, left_side=True, lower=True, trans...  9.93 us
    dot_general x1, matrix products, on_device(): jnp.einsum('liw,lwr->lir', own_grads, right_factor.astype(jnp.bfloat16),...  9.56 us
    dot_general x1, matrix products, on_device(): jnp.einsum('liw,lir->lwr', own_grads, small_left, preferred_element_type=...  8.11 us
    dot_general x1, matrix products, on_device(): jnp.einsum('lir,lrw->liw', left, mixed, precision=lax.Precision.HIGHEST)  7.16 us
  transfers between devices with their start and end apart: 2, of which 2 were waited for; matrix products, arithmetic and copies ran while one was open for 4% of the time, Pallas kernels for 0%

commit v1 on v0

--- a/solution.py
+++ b/solution.py
@@ -21,7 +21,7 @@
     part_right = jnp.einsum(
         "liw,lir->lwr", own_grads, small_left, preferred_element_type=jnp.float32
     )
-    right = lax.psum(part_right, ("dp", "tp"))
+    right = jnp.sum(lax.all_gather(part_right, ("dp", "tp")), axis=0)
     gram = gram + 0.001 * jnp.mean(jnp.diagonal(gram, axis1=1, axis2=2), axis=1)[
         :, None, None
     ] * jnp.eye(RANK, dtype=jnp.float32)

time: 276 us -> 260 us (0.942)
  waiting for transfers between devices: 196 us -> 176 us
  other arithmetic: 25.3 us -> 31.1 us
    psum x1 -> x0, waiting for transfers between devices: 120 us -> none  [on_device(): right = lax.psum(part_right, ('dp', 'tp'))]
    all_gather x0 -> x1, waiting for transfers between devices: none -> 99.2 us  [on_device(): right = jnp.sum(lax.all_gather(part_right, ('dp', 'tp')), axis=0)]
    reduce_sum x0 -> x1, other arithmetic: none -> 8 us  [on_device(): right = jnp.sum(lax.all_gather(part_right, ('dp', 'tp')), axis=0)]
  transfers between devices with their start and end apart: 2 -> 2, of which waited for: 2 -> 2; matrix products, arithmetic and copies ran while one was open for 4% -> 9% of each run, Pallas kernels for 0% -> 0%
where the time goes in v1:
time: 260 us; the launch traced here: 259 us
  waiting for transfers between devices  176 us (68%)
  other arithmetic  31.1 us (12%)
  matrix products  26.2 us (10%)
  between operations  14.1 us (5%)
  blocking collectives  10.7 us (4%)
    all_gather x1, waiting for transfers between devices, on_device(): right = jnp.sum(lax.all_gather(part_right, ('dp', 'tp')), axis=0)  99.2 us
    psum x1, waiting for transfers between devices, on_device(): left = lax.psum(part_left, 'dp')  76.5 us
    another operation x4, other arithmetic, on_device(): root = jnp.linalg.cholesky(gram)  11.9 us
    psum x1, blocking collectives, on_device(): gram = lax.psum(part_gram, 'tp')  10.7 us
    another operation x3, other arithmetic, on_device(): lax.linalg.triangular_solve(root, half, left_side=True, lower=True, trans...  9.94 us
    dot_general x1, matrix products, on_device(): jnp.einsum('liw,lwr->lir', own_grads, right_factor.astype(jnp.bfloat16),...  9.56 us
    dot_general x1, matrix products, on_device(): jnp.einsum('liw,lir->lwr', own_grads, small_left, preferred_element_type=...  8.14 us
    reduce_sum x1, other arithmetic, on_device(): right = jnp.sum(lax.all_gather(part_right, ('dp', 'tp')), axis=0)  8 us
  transfers between devices with their start and end apart: 2, of which 2 were waited for; matrix products, arithmetic and copies ran while one was open for 9% of the time, Pallas kernels for 0%

profile of v1, /device:TPU:0, one launch (start us, length us, event | category | flops | bytes accessed | tf_op | source)
XLA Modules:
  0.0 259.3 jit_solution(10151664990098252630)
XLA Ops:
  7.2 0.0 all-reduce.2.cloned.1.call-start
  7.2 9.6 %fusion.2 = f32[4,1280,32]{1,2,0:T(8,128)} fusion(bf16[1,4,1280,1280]{3,2,1,0:T(8,128)(2,1)} %param.4, f32[4,1280,32]{1,2,0:T(8,128)} %param.5), kind=kOutput, calls=%fused_computation.3 | convolution fusion | flops 419594240 | bytes 14417920 | tf_op jit(solution)/shard_map/liw,lwr->lir/dot_general | solution.py:11
  16.8 0.0 all-gather.3.cloned.1.call-start
  16.8 76.5 %all-reduce.2.cloned.1.call-done = f32[4,1280,32]{1,2,0:T(8,128)} async-done(((f32[4,1280,32]{1,2,0:T(8,128)}), f32[4,1280,32]{1,2,0:T(8,128)}) %all-reduce.2.cloned.1.call-update) | async-done | bytes 655376 | tf_op jit(solution)/shard_map/psum | solution.py:17
  93.3 8.1 %fusion.5 = f32[4,1280,32]{1,2,0:T(8,128)} fusion(bf16[1,4,1280,1280]{3,2,1,0:T(8,128)(2,1)} %param.4, f32[4,1280,32]{1,2,0:T(8,128)} %all-reduce.2.cloned.1.call-done), kind=kOutput, calls=%fused_computation.8 | convolution fusion | flops 419594240 | bytes 14417920 | tf_op jit(solution)/shard_map/liw,lir->lwr/dot_general | solution.py:21
  101.5 0.1 copy.17
  101.6 0.7 fusion.18
  102.3 10.7 %psum.15 = f32[4,32,32]{1,2,0:T(8,128)S(1)} all-reduce(f32[4,32,32]{1,2,0:T(8,128)S(1)} %fusion.18), channel_id=1, replica_groups=mesh['dp'=8,'tp'=4] {'tp'}, use_global_device_ids=true, to_apply=%region_1.0 | all-reduce | flops 4096 | bytes 32768 | tf_op jit(solution)/shard_map/psum | solution.py:20
  113.0 0.5 copy.16
  113.5 0.7 gather_fusion
  114.3 0.1 multiply_add_fusion
  114.4 0.1 copy.18
  114.4 0.1 fusion.15
  114.5 11.7 %custom-call.9 = f32[4,32,32]{2,1,0:T(8,128)S(1)} custom-call(f32[4,32,32]{2,1,0:T(8,128)S(1)} %fusion.15), custom_call_target="Cholesky" | custom-call | tf_op jit(solution)/shard_map/jit(cholesky)/cholesky | solution.py:30
  126.3 0.1 compare_reduce_fusion
  126.4 0.1 select_bitcast_fusion
  126.5 9.8 %custom-call.10 = f32[4,1,32,32]{2,3,1,0:T(8,128)S(1)} custom-call(f32[4,1,32,32]{3,2,1,0:T(8,128)S(1)} %select_bitcast_fusion), custom_call_target="InvertDiagBlocksLowerTriangular" | custom-call | tf_op jit(solution)/shard_map/triangular_solve | solution.py:34
  136.3 99.2 %all-gather.3.cloned.1.call-done = f32[128,1280,32]{1,2,0:T(8,128)} async-done(((f32[4,1280,32]{1,2,0:T(8,128)}), f32[128,1280,32]{1,2,0:T(8,128)}) %all-gather.3.cloned.1.call-update) | async-done | bytes 20971536 | tf_op jit(solution)/shard_map/all_gather | solution.py:24
  235.6 8.0 %reduce_sum.28 = f32[4,1280,32]{1,2,0:T(8,128)S(1)} reduce(f32[32,4,1280,32]{2,3,1,0:T(8,128)} %bitcast.28, f32[]{:T(128)} %constant.68.clone.1), dimensions={0}, to_apply=%region_5.6 | reduce | flops 5079040 | bytes 21626884 | tf_op jit(solution)/shard_map/reduce_sum | solution.py:24
  243.6 0.2 multiply_reduce_fusion
  243.7 0.4 fusion.10
  244.1 0.3 fusion.12
  244.4 1.0 broadcast_multiply_fusion
  245.3 7.2 %multiply_subtract_fusion = (f32[4,1280,160]{1,2,0:T(8,128)}, f32[4,1280,160]{1,2,0:T(8,128)}) fusion(f32[4,1280,160]{1,2,0:T(8,128)} %param.6, f32[4,1280,32]{1,2,0:T(8,128)S(1)} %copy-done, f32[4,32,160]{2,1,0:T(8,128)S(1)} %fusion.12, f32[4,1280,160]{1,2,0:T(8,128)} %param.7), kind=kOutput, calls=%fused_computation.7 | convolution fusion | flops 318668800 | bytes 13844480 | tf_op jit(solution)/shard_map/lir,lrw->liw/dot_general | solution.py:35
  (12 shorter events, 0.1 us)
Async XLA Ops:
  7.2 86.2 %all-reduce.2.cloned.1.call-start = ((), (), s32[]{:S(2)}) async-start(), calls=%async_computation | async-start | bytes 1310720 | tf_op jit(solution)/shard_map/psum | solution.py:17
  16.8 218.8 %all-gather.3.cloned.1.call-start = ((), (), s32[]{:S(2)}) async-start(), calls=%async_computation.1 | async-start | bytes 21626880 | tf_op jit(solution)/shard_map/all_gather | solution.py:24
  93.3 8.3 %copy-start = (f32[4,1280,32]{1,2,0:T(8,128)S(1)}, f32[4,1280,32]{1,2,0:T(8,128)}, u32[]{:S(2)}) copy-start(f32[4,1280,32]{1,2,0:T(8,128)} %all-reduce.2.cloned.1.call-done) | copy-start | bytes 1966084
Sparse Core Ops, SparseCore 0:
  16.9 76.3 all-reduce.1
  101.6 133.9 all-gather.2
